TPU v7x, 32 devices: a whole 2x2x4 slice. The times are simulated.
32 devices in a mesh: seq: 8 (over z, y), head: 4 (over x, core).
Axes of the slice: x: 2, y: 2, z: 4, core: 2. Of those that a mesh axis runs over, the one named last changes fastest.
Arguments:
- query_rows: bfloat16 [8192, 4096], P('seq', 'head'), may hold values from -6 to 6
- key_rows: bfloat16 [8192, 4096], P('seq', 'head'), may hold values from -6 to 6
- value_rows: bfloat16 [8192, 4096], P('seq', 'head'), may hold values from -15 to 15
- block_picks: int32 [16, 32, 4], P('seq', 'head'), may hold values from -1 to 15, as said below
- out_weight: bfloat16 [4096, 4096], P(None, 'head'), may hold values from -0.09375 to 0.09375
Outputs:
- mixed: bfloat16 [8192, 4096], P('seq', 'head')
Inputs may be any that keep to these rules, and one draw needn't show every extreme that they name: `block_picks`: every entry that is not -1 names a block held by a lower index of seq than block b. Repeated entries of one row count once. Over the query blocks of one index of seq and the heads of one index of head, at most 2 entries name blocks of any one other index of seq, and every index of seq from 1 on has exactly 2 entries naming blocks of index 0.
All inputs are finite; a program needn't handle non-finite values.
Results may differ from a plain program's by a relative error of at most 0.0059.
Values may be sent and summed in bfloat16 or wider, within the bound.
A program may use at most 192 MiB of HBM per device.

v0:
```python
import functools
import math

import jax
import jax.numpy as jnp
from jax import lax
from jax.experimental import pallas as pl
from jax.experimental.pallas import tpu as pltpu
from jax.sharding import PartitionSpec as P

CAP = 2
MESH = pl.DeviceIdType.MESH
F32 = jnp.float32
BF16 = jnp.bfloat16


def loop(lower, upper, step):
    def body(i, carry):
        step(i)
        return carry

    lax.fori_loop(lower, upper, body, 0)


def attend(query, key, value, causal_start=None):
    scale = query.shape[-1] ** -0.5
    scores = lax.dot_general(
        key, query, (((1,), (1,)), ((), ())), preferred_element_type=F32
    )
    if causal_start is not None:
        key_at = lax.broadcasted_iota(jnp.int32, scores.shape, 0)
        query_at = lax.broadcasted_iota(jnp.int32, scores.shape, 1) + causal_start
        scores = jnp.where(key_at <= query_at, scores, -jnp.inf)
    top = jnp.max(scores, axis=0, keepdims=True)
    weights = jnp.exp2((scores - top) * (scale * math.log2(math.e)))
    total = jnp.sum(weights, axis=0, keepdims=True)
    part = lax.dot_general(
        value, weights.astype(BF16), (((0,), (0,)), ((), ())), preferred_element_type=F32
    )
    return part / total, top * scale + jnp.log(total)


def plan_kernel(dims, picks, q, ask, slot, q_send, owner):
    n_seq, n_head, blocks, heads, n_pick, rows, width = dims
    pairs = blocks * heads
    me = lax.axis_index("seq")

    def find_owner(p):
        b, h = lax.div(p, heads), lax.rem(p, heads)
        found = [picks[b, h, t] for t in range(n_pick)]
        for t in range(n_pick):
            fresh = found[t] >= 0
            for earlier in range(t):
                fresh = fresh & (found[t] != found[earlier])
            owner[p * n_pick + t] = jnp.where(fresh, lax.div(found[t], blocks), -1)
            slot[p * n_pick + t] = -1

    loop(0, pairs, find_owner)

    def fill(s):
        def scan(p, carry):
            count, first, second = carry
            for t in range(n_pick):
                e = p * n_pick + t
                hit = owner[e] == s
                slot[e] = jnp.where(hit, s * CAP + count, slot[e])
                first = jnp.where(hit & (count == 0), e, first)
                second = jnp.where(hit & (count == 1), e, second)
                count = jnp.where(hit, count + 1, count)
            return count, first, second

        zero = jnp.int32(0)
        _, first, second = lax.fori_loop(0, pairs, scan, (zero, zero, zero))
        for c, e in enumerate((first, second)):
            p = lax.div(e, n_pick)
            pick = jnp.maximum(picks[lax.div(p, heads), lax.rem(p, heads), lax.rem(e, n_pick)], 0)
            ask[s, c] = lax.rem(pick, blocks) * heads + lax.rem(p, heads)
            q_send[s * CAP + c] = q[
                pl.ds(pl.multiple_of(lax.div(p, heads) * rows, rows), rows),
                pl.ds(pl.multiple_of(lax.rem(p, heads) * width, width), width),
            ]

    loop(0, me, fill)


def kernel(
    dims,
    q_hbm,
    k_hbm,
    v_hbm,
    ask,
    slot,
    q_send,
    w_hbm,
    out,
    q,
    k,
    v,
    w,
    asked,
    q_recv,
    o_send,
    o_recv,
    l_send,
    l_recv,
    own_o,
    own_l,
    gath,
    acc,
    load_sem,
    w_sem,
    ask_sem,
    qs_sem,
    os_sem,
    ls_sem,
    near_sem,
    cross_sem,
    fwd_sem,
):
    n_seq, n_head, blocks, heads, n_pick, rows, width = dims
    pairs = blocks * heads
    n_x = n_head // 2
    me = lax.axis_index("seq")
    hd = lax.axis_index("head")
    hx, hc = lax.div(hd, 2), lax.rem(hd, 2)
    mate = hx * 2 + 1 - hc

    def across(step):
        return lax.rem(hx + step, n_x) * 2 + hc

    def behind(step):
        return lax.rem(hx + n_x - step, n_x) * 2 + hc

    def load(i, p):
        src, dst = ((q_hbm, q), (k_hbm, k), (v_hbm, v))[i]
        b, h = lax.div(p, heads), lax.rem(p, heads)
        return pltpu.make_async_copy(
            src.at[
                pl.ds(pl.multiple_of(b * rows, rows), rows),
                pl.ds(pl.multiple_of(h * width, width), width),
            ],
            dst.at[p],
            load_sem.at[i, p],
        )

    def start_loads(p):
        for i in range(3):
            load(i, p).start()

    def end_loads(p):
        for i in range(3):
            load(i, p).wait()

    weight_load = pltpu.make_async_copy(w_hbm, w, w_sem.at[0])
    loop(0, pairs, start_loads)
    weight_load.start()

    barrier = pltpu.get_barrier_semaphore()

    def greet(d):
        pl.semaphore_signal(
            barrier, inc=1, device_id={"seq": lax.rem(me + d, n_seq)}, device_id_type=MESH
        )

    loop(1, n_seq, greet)
    for d in range(1, n_head):
        pl.semaphore_signal(
            barrier, inc=1, device_id={"head": lax.rem(hd + d, n_head)}, device_id_type=MESH
        )

    pl.semaphore_wait(barrier, n_seq + n_head - 2)

    def ask_copy(s, r):
        return pltpu.make_async_remote_copy(
            src_ref=ask.at[s],
            dst_ref=asked.at[r],
            send_sem=ask_sem.at[0, s],
            recv_sem=ask_sem.at[1, r],
            device_id={"seq": s},
            device_id_type=MESH,
        )

    def q_copy(s, r):
        return pltpu.make_async_remote_copy(
            src_ref=q_send.at[pl.ds(s * CAP, CAP)],
            dst_ref=q_recv.at[pl.ds(r * CAP, CAP)],
            send_sem=qs_sem.at[0, s],
            recv_sem=qs_sem.at[1, r],
            device_id={"seq": s},
            device_id_type=MESH,
        )

    def o_copy(r, s):
        return pltpu.make_async_remote_copy(
            src_ref=o_send.at[pl.ds(r * CAP, CAP)],
            dst_ref=o_recv.at[pl.ds(s * CAP, CAP)],
            send_sem=os_sem.at[0, r],
            recv_sem=os_sem.at[1, s],
            device_id={"seq": r},
            device_id_type=MESH,
        )

    def l_copy(r, s):
        return pltpu.make_async_remote_copy(
            src_ref=l_send.at[pl.ds(r * CAP, CAP)],
            dst_ref=l_recv.at[pl.ds(s * CAP, CAP)],
            send_sem=ls_sem.at[0, r],
            recv_sem=ls_sem.at[1, s],
            device_id={"seq": r},
            device_id_type=MESH,
        )

    def send_queries(s):
        ask_copy(s, me).start()
        q_copy(s, me).start()

    loop(0, me, send_queries)
    loop(0, pairs, end_loads)

    half = rows // 2

    def own(p):
        query, key, value = q[p], k[p], v[p]
        for part in range(2):
            seen = (part + 1) * half
            span = slice(part * half, seen)
            result, level = attend(query[span], key[:seen], value[:seen], part * half)
            own_o[p, :, span] = result
            own_l[p, :, span] = level

    def serve(r):
        ask_copy(me, r).wait_recv()
        q_copy(me, r).wait_recv()

        def one(c):
            code = asked[r, c]
            query, key, value = q_recv[r * CAP + c], k[code], v[code]
            for part in range(2):
                span = slice(part * half, (part + 1) * half)
                result, level = attend(query[span], key, value)
                o_send[r * CAP + c, :, span] = result.astype(BF16)
                l_send[r * CAP + c, :, span] = level

        loop(0, CAP, one)
        o_copy(r, me).start()
        l_copy(r, me).start()

    served = n_seq - 1 - me
    ahead = jnp.minimum(pairs, 4 * (me + 1))

    def round_of(t):
        lower = jnp.where(t == 0, 0, jnp.minimum(pairs, ahead + 2 * (t - 1)))
        upper = jnp.where(t == served, pairs, jnp.minimum(pairs, ahead + 2 * t))
        loop(lower, upper, own)

        @pl.when(t < served)
        def _():
            serve(n_seq - 1 - t)

    loop(0, served + 1, round_of)

    def collect(s):
        o_copy(s, s).wait_recv()
        l_copy(s, s).wait_recv()

    loop(0, me, collect)

    groups = heads // 2
    chunks = blocks * groups

    def head_copy(src, dst, sems, index, target):
        return pltpu.make_async_remote_copy(
            src_ref=gath.at[src, index],
            dst_ref=gath.at[dst, index],
            send_sem=sems[0],
            recv_sem=sems[1],
            device_id={"head": target},
            device_id_type=MESH,
        )

    def near_copy(index):
        return head_copy(hd, hd, (near_sem.at[0, index], near_sem.at[1, index]), index, mate)

    def cross_copy(step, index):
        sems = (cross_sem.at[0, step - 1, index], cross_sem.at[1, step - 1, index])
        return head_copy(hd, hd, sems, index, across(step))

    def fwd_copy(step, index):
        sems = (fwd_sem.at[0, step - 1, index], fwd_sem.at[1, step - 1, index])
        return head_copy(behind(step), behind(step), sems, index, mate)

    def merge(p):
        level = own_l[p]
        levels, slots = [], []
        for t in range(n_pick):
            at = slot[p * n_pick + t]
            safe = jnp.maximum(at, 0)
            far = l_recv[safe]
            levels.append(jnp.where(at >= 0, far, -jnp.inf))
            slots.append((at, safe))
        largest = level
        for far in levels:
            largest = jnp.maximum(largest, far)
        factor = jnp.exp(level - largest)
        denom = factor
        factors = []
        for far in levels:
            factors.append(jnp.exp(far - largest))
            denom = denom + factors[-1]
        numer = (factor / denom) * own_o[p]
        for (at, safe), far in zip(slots, factors):
            part = o_recv[safe].astype(F32)
            numer = numer + jnp.where(at >= 0, (far / denom) * part, 0.0)
        return numer.T.astype(BF16)

    def merge_group(index):
        for i in range(2):
            gath[hd, index, :, i * width : (i + 1) * width] = merge(index * 2 + i)
        for step in range(1, n_x):
            cross_copy(step, index).start()
        near_copy(index).start()

    loop(0, chunks, merge_group)
    weight_load.wait()

    depth = 2 * width

    def project(source, index, fresh=False):
        b, g = lax.div(index, groups), lax.rem(index, groups)
        at = pl.multiple_of((source * groups + g) * depth, depth)
        result = jnp.dot(
            gath[source, index], w[pl.ds(at, depth), :], preferred_element_type=F32
        )
        if fresh:
            acc[b] = result
        else:
            acc[b] += result

    def start_rows(b):
        acc[b] = jnp.zeros(acc.shape[1:], F32)

    loop(0, blocks, start_rows)
    loop(0, chunks, lambda index: project(hd, index))

    def take_near(index):
        near_copy(index).wait_recv()
        project(mate, index)

    loop(0, chunks, take_near)

    for step in range(1, n_x):

        def take_cross(index):
            cross_copy(step, index).wait_recv()
            fwd_copy(step, index).start()
            project(behind(step), index)
            fwd_copy(step, index).wait_recv()
            project(lax.rem(hx + n_x - step, n_x) * 2 + 1 - hc, index)

        loop(0, chunks, take_cross)

    def finish(b):
        out[pl.ds(pl.multiple_of(b * rows, rows), rows), :] = acc[b].astype(BF16)

    loop(0, blocks, finish)

    def sent_queries(s):
        ask_copy(s, me).wait_send()
        q_copy(s, me).wait_send()

    loop(0, me, sent_queries)

    def sent_results(r):
        o_copy(r, me).wait_send()
        l_copy(r, me).wait_send()

    loop(me + 1, n_seq, sent_results)

    def sent_heads(index):
        near_copy(index).wait_send()
        for step in range(1, n_x):
            cross_copy(step, index).wait_send()
            fwd_copy(step, index).wait_send()

    loop(0, chunks, sent_heads)


def solution(mesh):
    n_seq, n_head = mesh.shape["seq"], mesh.shape["head"]

    def body(query_rows, key_rows, value_rows, block_picks, out_weight):
        tok_rows, feature_width = query_rows.shape
        blocks, heads, n_pick = block_picks.shape
        rows, width = tok_rows // blocks, feature_width // heads
        pairs = blocks * heads
        chunks = pairs // 2
        n_x = n_head // 2
        any_spec = pl.BlockSpec(memory_space=pl.ANY)
        smem_spec = pl.BlockSpec(memory_space=pltpu.SMEM)
        vmem_spec = pl.BlockSpec(memory_space=pltpu.VMEM)
        out_width = out_weight.shape[1]
        slots = n_seq * CAP
        dma = pltpu.SemaphoreType.DMA
        dims = (n_seq, n_head, blocks, heads, n_pick, rows, width)
        ask, slot, q_send = pl.pallas_call(
            functools.partial(plan_kernel, dims),
            out_shape=(
                jax.ShapeDtypeStruct((n_seq, CAP), jnp.int32),
                jax.ShapeDtypeStruct((pairs * n_pick,), jnp.int32),
                jax.ShapeDtypeStruct((slots, rows, width), BF16),
            ),
            in_specs=[smem_spec, vmem_spec],
            out_specs=(smem_spec, smem_spec, vmem_spec),
            scratch_shapes=[pltpu.SMEM((pairs * n_pick,), jnp.int32)],
            name="plan",
        )(block_picks, query_rows)
        return pl.pallas_call(
            functools.partial(kernel, dims),
            out_shape=jax.ShapeDtypeStruct((tok_rows, out_width), BF16),
            in_specs=[any_spec] * 3 + [smem_spec] * 2 + [any_spec] * 2,
            out_specs=vmem_spec,
            scratch_shapes=[
                pltpu.VMEM((pairs, rows, width), BF16),
                pltpu.VMEM((pairs, rows, width), BF16),
                pltpu.VMEM((pairs, rows, width), BF16),
                pltpu.VMEM(out_weight.shape, BF16),
                pltpu.SMEM((n_seq, CAP), jnp.int32),
                pltpu.VMEM((slots, rows, width), BF16),
                pltpu.VMEM((slots, width, rows), BF16),
                pltpu.VMEM((slots, width, rows), BF16),
                pltpu.VMEM((slots, 1, rows), F32),
                pltpu.VMEM((slots, 1, rows), F32),
                pltpu.VMEM((pairs, width, rows), F32),
                pltpu.VMEM((pairs, 1, rows), F32),
                pltpu.VMEM((n_head, chunks, rows, 2 * width), BF16),
                pltpu.VMEM((blocks, rows, out_width), F32),
                dma((3, pairs)),
                dma((1,)),
                dma((2, n_seq)),
                dma((2, n_seq)),
                dma((2, n_seq)),
                dma((2, n_seq)),
                dma((2, chunks)),
                dma((2, max(n_x - 1, 1), chunks)),
                dma((2, max(n_x - 1, 1), chunks)),
            ],
            compiler_params=pltpu.CompilerParams(
                collective_id=0,
                has_side_effects=True,
                vmem_limit_bytes=67043328,
            ),
            name="layer",
        )(query_rows, key_rows, value_rows, ask, slot, q_send, out_weight)

    return jax.shard_map(
        body,
        mesh=mesh,
        in_specs=(
            P("seq", "head"),
            P("seq", "head"),
            P("seq", "head"),
            P("seq", "head", None),
            P(None, "head"),
        ),
        out_specs=P("seq", "head"),
        check_vma=False,
    )
```

profile of v0, /device:TPU:17, one launch (start us, length us, event | category | flops | bytes accessed | tf_op | source)
XLA Modules:
  0.0 130.4 jit_solution(12195770373680383626)
XLA Ops:
  0.0 1.4 %copy.6.picks = s32[2,8,4]{2,1,0:T(8,128)} copy(s32[2,8,4]{1,2,0:T(4,128)} %param.8) | data formatting | bytes 512 | tf_op args[3]
  1.4 5.1 %plan.1 = (s32[8,2]{1,0:T(8,128)}, s32[64]{0:T(128)}, bf16[16,512,128]{2,1,0:T(8,128)(2,1)}) custom-call(s32[2,8,4]{2,1,0:T(8,128)} %copy.6.picks, bf16[1024,1024]{1,0:T(8,128)(2,1)} %q_hbm.1), custom_call_target="tpu_custom_call" | custom-call | tf_op jit(solution)/shard_map/plan/pallas_call | solution.py:405
  6.4 120.9 %layer.1 = bf16[1024,1024]{1,0:T(8,128)(2,1)} custom-call(bf16[1024,1024]{1,0:T(8,128)(2,1)} %q_hbm.1, bf16[1024,1024]{1,0:T(8,128)(2,1)} %k_hbm.1, bf16[1024,1024]{1,0:T(8,128)(2,1)} %v_hbm.1, s32[8,2]{1,0:T(8,128)} %get-tuple-element.8.ask, s32[64]{0:T(128)} %get-tuple-element.9.slot, bf16[16,512,128]{2,1,0:T(8,128)(2,1)} %get-tuple-element.10.q_send, ...), custom_call_target="tpu_custom_call" | custom-call | tf_op jit(solution)/shard_map/layer/pallas_call | solution.py:417
  127.3 3.1 %copy.8 = bf16[1024,1024]{1,0:T(8,128)(2,1)} copy(bf16[1024,1024]{1,0:T(8,128)(2,1)} %layer.1) | data formatting | bytes 4194304
where the time goes:
time: 131 us; the launch traced here: 130 us
  Pallas kernels  126 us (96%)
  local copies, waits for them, and re-layouts  4.43 us (3%)
    pallas_call x1, Pallas kernels, body(): pl.pallas_call(functools.partial(kernel, dims), out_shape=jax.ShapeDtypeS...  121 us
    pallas_call x1, Pallas kernels, body(): pl.pallas_call(functools.partial(plan_kernel, dims), out_shape=(jax.Shape...  5.08 us
    unnamed x2, local copies, waits for them, and re-layouts  4.43 us

commit v1 on v0

v1 whole, which is shorter than its diff:
```python
import functools
import math

import jax
import jax.numpy as jnp
from jax import lax
from jax.experimental import pallas as pl
from jax.experimental.pallas import tpu as pltpu
from jax.sharding import PartitionSpec as P

CAP = 2
MESH = pl.DeviceIdType.MESH
F32 = jnp.float32
BF16 = jnp.bfloat16


def loop(lower, upper, step):
    def body(i, carry):
        step(i)
        return carry

    lax.fori_loop(lower, upper, body, 0)


def attend(query, key, value, causal_start=None):
    scale = query.shape[-1] ** -0.5
    scores = lax.dot_general(
        key, query, (((1,), (1,)), ((), ())), preferred_element_type=F32
    )
    if causal_start is not None:
        key_at = lax.broadcasted_iota(jnp.int32, scores.shape, 0)
        query_at = lax.broadcasted_iota(jnp.int32, scores.shape, 1) + causal_start
        scores = jnp.where(key_at <= query_at, scores, -jnp.inf)
    top = jnp.max(scores, axis=0, keepdims=True)
    weights = jnp.exp2((scores - top) * (scale * math.log2(math.e)))
    total = jnp.sum(weights, axis=0, keepdims=True)
    part = lax.dot_general(
        value, weights.astype(BF16), (((0,), (0,)), ((), ())), preferred_element_type=F32
    )
    return part / total, top * scale + jnp.log(total)


def kernel(
    dims,
    q_hbm,
    k_hbm,
    v_hbm,
    picks,
    w_hbm,
    out,
    q,
    k,
    v,
    w,
    owner,
    first,
    tile_at,
    ask,
    asking,
    asked,
    order,
    orders,
    q_out,
    q_in,
    o_out,
    o_in,
    l_out,
    l_in,
    o_all,
    l_all,
    own_g,
    mate_g,
    cross_g,
    fwd_g,
    acc,
    load_sem,
    w_sem,
    ask_sem,
    order_sem,
    q_sem,
    o_sem,
    l_sem,
    near_sem,
    cross_sem,
    fwd_sem,
):
    n_seq, n_head, blocks, heads, n_pick, rows, width = dims
    pairs = blocks * heads
    n_x = n_head // 2
    me = lax.axis_index("seq")
    hd = lax.axis_index("head")
    hx, hc = lax.div(hd, 2), lax.rem(hd, 2)
    mate = hx * 2 + 1 - hc
    half = rows // 2
    n_tiles = me * CAP
    n_serve = (n_seq - 1 - me) * CAP
    free = jnp.maximum(pairs - n_tiles, 0)
    odd = lax.rem(me, 2)
    lines, line = n_seq // 2, lax.div(me, 2)
    middle = lines // 2

    def across(step):
        return lax.rem(hx + step, n_x) * 2 + hc

    def behind(step):
        return lax.rem(hx + n_x - step, n_x) * 2 + hc

    def load(i, p):
        src, dst = ((q_hbm, q), (k_hbm, k), (v_hbm, v))[i]
        b, h = lax.div(p, heads), lax.rem(p, heads)
        return pltpu.make_async_copy(
            src.at[
                pl.ds(pl.multiple_of(b * rows, rows), rows),
                pl.ds(pl.multiple_of(h * width, width), width),
            ],
            dst.at[p],
            load_sem.at[i, p],
        )

    weight_load = pltpu.make_async_copy(w_hbm, w, w_sem.at[0])
    loop(0, pairs, lambda p: load(0, p).start())

    barrier = pltpu.get_barrier_semaphore()

    def greet(d):
        pl.semaphore_signal(
            barrier, inc=1, device_id={"seq": lax.rem(me + d, n_seq)}, device_id_type=MESH
        )

    loop(1, n_seq, greet)
    for d in range(1, n_head):
        pl.semaphore_signal(
            barrier, inc=1, device_id={"head": lax.rem(hd + d, n_head)}, device_id_type=MESH
        )

    for i in range(1, 3):
        loop(0, pairs, lambda p, i=i: load(i, p).start())

    def find_owner(p):
        b, h = lax.div(p, heads), lax.rem(p, heads)
        found = [picks[b, t, h] for t in range(n_pick)]
        for t in range(n_pick):
            fresh = found[t] >= 0
            for earlier in range(t):
                fresh = fresh & (found[t] != found[earlier])
            owner[p * n_pick + t] = jnp.where(fresh, lax.div(found[t], blocks), -1)

    loop(0, pairs, find_owner)

    def clear(s):
        first[s] = 0

    loop(0, n_seq, clear)

    def find_asks(d):
        s = me - 1 - d

        def scan(p, carry):
            low, high = carry
            for t in range(n_pick):
                e = p * n_pick + t
                hit = owner[e] == s
                low = jnp.minimum(low, jnp.where(hit, e, pairs * n_pick))
                high = jnp.maximum(high, jnp.where(hit, e, 0))
            return low, high

        low, high = lax.fori_loop(0, pairs, scan, (jnp.int32(pairs * n_pick), jnp.int32(0)))
        first[s] = low
        for c, e in enumerate((jnp.where(low < pairs * n_pick, low, 0), high)):
            p = lax.div(e, n_pick)
            b, h = lax.div(p, heads), lax.rem(p, heads)
            pick = jnp.maximum(picks[b, lax.rem(e, n_pick), h], 0)
            ask[s, c] = lax.rem(pick, blocks) * heads + h
            asking[s, c] = p

    def ask_copy(s, r):
        return pltpu.make_async_remote_copy(
            src_ref=ask.at[s],
            dst_ref=asked.at[r],
            send_sem=ask_sem.at[0, s],
            recv_sem=ask_sem.at[1, r],
            device_id={"seq": s},
            device_id_type=MESH,
        )

    def tile_copy(source, landing, sems, there, here, target):
        return pltpu.make_async_remote_copy(
            src_ref=source.at[there],
            dst_ref=landing.at[here],
            send_sem=sems.at[0, there],
            recv_sem=sems.at[1, here],
            device_id={"seq": target},
            device_id_type=MESH,
        )

    def q_copy(s, r, c):
        return tile_copy(q_out, q_in, q_sem, s * CAP + c, r * CAP + c, s)

    def o_copy(r, s, c):
        return tile_copy(o_out, o_in, o_sem, r * CAP + c, s * CAP + c, r)

    def l_copy(r, s, c):
        return tile_copy(l_out, l_in, l_sem, r * CAP + c, s * CAP + c, r)

    def at_least(value, bound):
        return lax.div(value - bound + 4 * n_seq, 4 * n_seq)

    def pick(flag, yes, no):
        return flag * yes + (1 - flag) * no

    def source_of(n):
        lone = odd * CAP
        is_late = at_least(n, lone)
        late = (n - lone) * is_late
        group = lax.div(late, 2 * CAP)
        there = pick(downward, line - 1 - group, group)
        s = 2 * there + 1 - lax.rem(late, 2)
        c = lax.div(lax.rem(late, 2 * CAP), 2)
        return pick(is_late, s, me - 1), pick(is_late, c, n)

    def tile_of(s, c):
        there = lax.div(s, 2)
        group = pick(downward, line - 1 - there, there)
        late = odd * CAP + group * (2 * CAP) + c * 2 + 1 - lax.rem(s, 2)
        return jnp.where(there == line, c, late)

    downward = at_least(line, middle + 1)
    beyond = pick(downward, line, middle) + 1
    n_near = lines - beyond

    def requester_of(n):
        lone = (1 - odd) * CAP
        is_late = at_least(n, lone)
        late = (n - lone) * is_late
        group = lax.div(late, 2 * CAP)
        low = pick(at_least(group, middle), group + 1, middle - group)
        high = pick(at_least(group, n_near), line + 1 + group - n_near, beyond + group)
        r = 2 * pick(at_least(line, 1), high, low) + lax.rem(late, 2)
        c = lax.div(lax.rem(late, 2 * CAP), 2)
        return pick(is_late, r, me + 1), pick(is_late, c, n)

    def start_rows(b):
        acc[b] = jnp.zeros(acc.shape[1:], F32)

    loop(0, me, find_asks)
    loop(0, blocks, start_rows)
    loop(0, pairs, lambda p: load(0, p).wait())

    def stage(n):
        s, c = source_of(n)
        q_out[s * CAP + c] = q[asking[s, c]]

    def send(n):
        s, c = source_of(n)

        @pl.when(c == 0)
        def _():
            ask_copy(s, me).start()

        q_copy(s, me, c).start()

    loop(0, n_tiles, stage)
    pl.semaphore_wait(barrier, n_seq + n_head - 2)
    loop(0, n_tiles, send)

    def place(p):
        key = jnp.int32(-1)
        for t in range(n_pick):
            e = p * n_pick + t
            s = owner[e]
            c = jnp.where(first[jnp.maximum(s, 0)] == e, 0, 1)
            at = jnp.where(s >= 0, tile_of(s, c), -1)
            tile_at[e] = at
            key = jnp.maximum(key, at)
        owner[p * n_pick] = key * pairs + p

    loop(0, pairs, place)

    def rank(p):
        key = owner[p * n_pick]
        ahead = jnp.int32(0)
        for other in range(pairs):
            ahead = ahead + jnp.where(owner[other * n_pick] < key, 1, 0)
        order[1, p] = ahead

    loop(0, pairs, rank)

    def invert(i):
        found = jnp.int32(0)
        for p in range(pairs):
            found = found + jnp.where(order[1, p] == i, p, 0)
        order[0, i] = found

    loop(0, pairs, invert)

    def order_copy(d):
        target = lax.rem(hd + d, n_head)
        return pltpu.make_async_remote_copy(
            src_ref=order,
            dst_ref=orders.at[hd],
            send_sem=order_sem.at[0, d],
            recv_sem=order_sem.at[1, hd],
            device_id={"head": target},
            device_id_type=MESH,
        )

    def order_wait(d):
        source = lax.rem(hd + d, n_head)
        return pltpu.make_async_remote_copy(
            src_ref=order,
            dst_ref=orders.at[source],
            send_sem=order_sem.at[0, d],
            recv_sem=order_sem.at[1, source],
            device_id={"head": source},
            device_id_type=MESH,
        )

    for d in range(1, n_head):
        order_copy(d).start()

    for i in range(1, 3):
        loop(0, pairs, lambda p, i=i: load(i, p).wait())
    weight_load.start()

    def head_copy(src, dst, sems, target):
        return pltpu.make_async_remote_copy(
            src_ref=src,
            dst_ref=dst,
            send_sem=sems[0],
            recv_sem=sems[1],
            device_id={"head": target},
            device_id_type=MESH,
        )

    def near_copy(i):
        sems = (near_sem.at[0, i], near_sem.at[1, i])
        return head_copy(own_g.at[i], mate_g.at[i], sems, mate)

    def cross_copy(step, i):
        sems = (cross_sem.at[0, step - 1, i], cross_sem.at[1, step - 1, i])
        return head_copy(own_g.at[i], cross_g.at[step - 1, i], sems, across(step))

    def fwd_copy(step, i):
        sems = (fwd_sem.at[0, step - 1, i], fwd_sem.at[1, step - 1, i])
        return head_copy(cross_g.at[step - 1, i], fwd_g.at[step - 1, i], sems, mate)

    def merge(p, span, part, level):
        levels, tiles = [], []
        for t in range(n_pick):
            at = tile_at[p * n_pick + t]
            safe = jnp.maximum(at, 0)
            levels.append(jnp.where(at >= 0, l_all[safe, :, span], -jnp.inf))
            tiles.append((at, safe))
        largest = level
        for far in levels:
            largest = jnp.maximum(largest, far)
        factor = jnp.exp(level - largest)
        denom = factor
        factors = []
        for far in levels:
            factors.append(jnp.exp(far - largest))
            denom = denom + factors[-1]
        numer = (factor / denom) * part
        for (at, safe), far in zip(tiles, factors):
            far_part = o_all[safe, :, span].astype(F32)
            numer = numer + jnp.where(at >= 0, (far / denom) * far_part, 0.0)
        return numer

    def position(i, gated):
        p = order[0, i]
        query, key, value = q[p], k[p], v[p]
        for part in range(2):
            seen = (part + 1) * half
            span = slice(part * half, seen)
            result, level = attend(query[span], key[:seen], value[:seen], part * half)
            if gated:
                result = merge(p, span, result, level)
            own_g[i, span, :] = result.T.astype(BF16)
        for step in range(1, n_x):
            cross_copy(step, i).start()
        near_copy(i).start()

    def serve(n):
        r, c = requester_of(n)
        slot = r * CAP + c

        @pl.when(c == 0)
        def _():
            ask_copy(me, r).wait_recv()

        q_copy(me, r, c).wait_recv()
        code = asked[r, c]
        query, key, value = q_in[slot], k[code], v[code]
        for part in range(2):
            span = slice(part * half, (part + 1) * half)
            result, level = attend(query[span], key, value)
            o_out[slot, :, span] = result.astype(BF16)
            l_out[slot, :, span] = level
        l_copy(r, me, c).start()
        o_copy(r, me, c).start()

    def take_tile(n):
        s, c = source_of(n)
        l_copy(s, s, c).wait_recv()
        o_copy(s, s, c).wait_recv()
        o_all[n] = o_in[s * CAP + c]
        l_all[n] = l_in[s * CAP + c]

    def forward(i):
        for step in range(1, n_x):
            cross_copy(step, i).wait_recv()
            fwd_copy(step, i).start()

    def project(sources, places, tiles):
        weights = jnp.concatenate(
            [
                w[source * heads + lax.rem(p, heads)]
                for source, p in zip(sources, places)
            ],
            axis=0,
        )
        for b in range(blocks):
            seen = jnp.concatenate(
                [
                    jnp.where(lax.div(p, heads) == b, tile, jnp.zeros_like(tile))
                    for p, tile in zip(places, tiles)
                ],
                axis=1,
            )
            acc[b] += jnp.dot(seen, weights, preferred_element_type=F32)

    def project_near(i):
        near_copy(i).wait_recv()
        project((hd, mate), (order[0, i], orders[mate, 0, i]), (own_g[i], mate_g[i]))

    def project_far(i):
        for step in range(1, n_x):
            fwd_copy(step, i).wait_recv()
            from_x = behind(step)
            from_mate = lax.rem(hx + n_x - step, n_x) * 2 + 1 - hc
            project(
                (from_x, from_mate),
                (orders[from_x, 0, i], orders[from_mate, 0, i]),
                (cross_g[step - 1, i], fwd_g[step - 1, i]),
            )

    def pass_on(i):
        forward(i)
        project_near(i)

        @pl.when(i > 0)
        def _():
            project_far(i - 1)

    loop(0, free, lambda i: position(i, False))
    weight_load.wait()
    for d in range(1, n_head):
        order_wait(d).wait_recv()

    n_late = jnp.where(line > 0, jnp.maximum(middle - line, 0) * 2 * CAP, 0)
    n_soon = n_serve - n_late
    ready = jnp.maximum(free - 1, 0)

    def passed(n):
        return jnp.clip(n - 1 - me, 0, ready)

    def soon_step(n):
        serve(n)
        loop(passed(n - 1), passed(n), pass_on)

    loop(0, n_soon, soon_step)
    start = passed(n_soon - 1)

    def gate(i):
        return jnp.maximum(n_tiles - (pairs - 1 - i), 0)

    def passed_gated(i):
        return jnp.where((n_late > 0) | (i < free), start, jnp.maximum(i - 1, start))

    def gated_step(i):
        loop(jnp.where(i == free, 0, gate(i - 1)), gate(i), take_tile)
        position(i, True)
        loop(passed_gated(i - 1), passed_gated(i), pass_on)

    loop(free, pairs, gated_step)
    middle_pass = passed_gated(jnp.where(free < pairs, pairs - 1, free - 1))

    def passed_late(n):
        here = jnp.maximum(pairs - 3 - n_serve + n, middle_pass)
        return jnp.where(n < n_soon, middle_pass, jnp.clip(here, 0, pairs - 1))

    def late_step(n):
        loop(passed_late(n - 1), passed_late(n), pass_on)
        serve(n)

    loop(n_soon, n_serve, late_step)
    loop(passed_late(n_serve - 1), pairs - 1, pass_on)
    project_near(pairs - 1)
    forward(pairs - 1)
    loop(pairs - 2, pairs, project_far)

    def finish(b):
        out[pl.ds(pl.multiple_of(b * rows, rows), rows), :] = acc[b].astype(BF16)

    loop(0, blocks, finish)

    def sent_asks(s):
        ask_copy(s, me).wait_send()
        for c in range(CAP):
            q_copy(s, me, c).wait_send()

    loop(0, me, sent_asks)

    def sent_results(r):
        for c in range(CAP):
            o_copy(r, me, c).wait_send()
            l_copy(r, me, c).wait_send()

    loop(me + 1, n_seq, sent_results)
    for d in range(1, n_head):
        order_copy(d).wait_send()

    def sent_heads(i):
        near_copy(i).wait_send()
        for step in range(1, n_x):
            cross_copy(step, i).wait_send()
            fwd_copy(step, i).wait_send()

    loop(0, pairs, sent_heads)


def solution(mesh):
    n_seq, n_head = mesh.shape["seq"], mesh.shape["head"]

    def body(query_rows, key_rows, value_rows, block_picks, out_weight):
        tok_rows, feature_width = query_rows.shape
        blocks, heads, n_pick = block_picks.shape
        rows, width = tok_rows // blocks, feature_width // heads
        pairs = blocks * heads
        crossings = max(n_head // 2 - 1, 1)
        any_spec = pl.BlockSpec(memory_space=pl.ANY)
        smem_spec = pl.BlockSpec(memory_space=pltpu.SMEM)
        vmem_spec = pl.BlockSpec(memory_space=pltpu.VMEM)
        out_width = out_weight.shape[1]
        slots = n_seq * CAP
        dma = pltpu.SemaphoreType.DMA
        dims = (n_seq, n_head, blocks, heads, n_pick, rows, width)
        tiles = pltpu.VMEM((pairs, rows, width), BF16)
        return pl.pallas_call(
            functools.partial(kernel, dims),
            out_shape=jax.ShapeDtypeStruct((tok_rows, out_width), BF16),
            in_specs=[any_spec] * 3 + [smem_spec] + [any_spec],
            out_specs=vmem_spec,
            scratch_shapes=[
                tiles,
                tiles,
                tiles,
                pltpu.VMEM((out_weight.shape[0] // width, width, out_width), BF16),
                pltpu.SMEM((pairs * n_pick,), jnp.int32),
                pltpu.SMEM((n_seq,), jnp.int32),
                pltpu.SMEM((pairs * n_pick,), jnp.int32),
                pltpu.SMEM((n_seq, CAP), jnp.int32),
                pltpu.SMEM((n_seq, CAP), jnp.int32),
                pltpu.SMEM((n_seq, CAP), jnp.int32),
                pltpu.SMEM((2, pairs), jnp.int32),
                pltpu.SMEM((n_head, 2, pairs), jnp.int32),
                pltpu.VMEM((slots, rows, width), BF16),
                pltpu.VMEM((slots, rows, width), BF16),
                pltpu.VMEM((slots, width, rows), BF16),
                pltpu.VMEM((slots, width, rows), BF16),
                pltpu.VMEM((slots, 1, rows), F32),
                pltpu.VMEM((slots, 1, rows), F32),
                pltpu.VMEM((slots, width, rows), BF16),
                pltpu.VMEM((slots, 1, rows), F32),
                tiles,
                tiles,
                pltpu.VMEM((crossings, pairs, rows, width), BF16),
                pltpu.VMEM((crossings, pairs, rows, width), BF16),
                pltpu.VMEM((blocks, rows, out_width), F32),
                dma((3, pairs)),
                dma((1,)),
                dma((2, n_seq)),
                dma((2, n_head)),
                dma((2, slots)),
                dma((2, slots)),
                dma((2, slots)),
                dma((2, pairs)),
                dma((2, crossings, pairs)),
                dma((2, crossings, pairs)),
            ],
            compiler_params=pltpu.CompilerParams(
                collective_id=0,
                has_side_effects=True,
                vmem_limit_bytes=67043328,
            ),
            name="layer",
        )(query_rows, key_rows, value_rows, jnp.swapaxes(block_picks, 1, 2),
          out_weight.reshape(-1, width, out_width))

    return jax.shard_map(
        body,
        mesh=mesh,
        in_specs=(
            P("seq", "head"),
            P("seq", "head"),
            P("seq", "head"),
            P("seq", "head", None),
            P(None, "head"),
        ),
        out_specs=P("seq", "head"),
        check_vma=False,
    )
```

time: 131 us -> 93.9 us (0.72)
  the two profiles are of different devices: /device:TPU:17 before, /device:TPU:21 now
where the time goes in v1:
time: 93.9 us; the launch traced here: 93.7 us
  Pallas kernels  90.6 us (96%)
  local copies, waits for them, and re-layouts  3.08 us (3%)
    pallas_call x1, Pallas kernels, body(): pl.pallas_call(functools.partial(kernel, dims), out_shape=jax.ShapeDtypeS...  90.6 us
    unnamed x1, local copies, waits for them, and re-layouts  3.08 us

profile of v1, /device:TPU:21, one launch (start us, length us, event | category | flops | bytes accessed | tf_op | source)
XLA Modules:
  0.0 93.7 jit_solution(2957889781077491174)
XLA Ops:
  0.0 90.6 %layer.1 = bf16[1024,1024]{1,0:T(8,128)(2,1)} custom-call(bf16[1024,1024]{1,0:T(8,128)(2,1)} %q_hbm.1, bf16[1024,1024]{1,0:T(8,128)(2,1)} %k_hbm.1, bf16[1024,1024]{1,0:T(8,128)(2,1)} %v_hbm.1, s32[2,4,8]{2,1,0:T(4,128)} %bitcast.3, bf16[32,128,1024]{2,1,0:T(8,128)(2,1)} %bitcast.2), custom_call_target="tpu_custom_call" | custom-call | tf_op jit(solution)/shard_map/layer/pallas_call | solution.py:549
  90.7 3.1 %copy.7 = bf16[1024,1024]{1,0:T(8,128)(2,1)} copy(bf16[1024,1024]{1,0:T(8,128)(2,1)} %layer.1) | data formatting | bytes 4194304

commit v2 on v1

--- a/solution.py
+++ b/solution.py
@@ -228,16 +228,18 @@
     beyond = pick(downward, line, middle) + 1
     n_near = lines - beyond
 
+    lone_at = 2 * CAP * at_least(lines, line + 2) * at_least(line, middle)
+
     def requester_of(n):
-        lone = (1 - odd) * CAP
-        is_late = at_least(n, lone)
-        late = (n - lone) * is_late
+        past = (1 - odd) * at_least(n, lone_at + CAP)
+        is_lone = (1 - odd) * at_least(n, lone_at) - past
+        late = (n - past * CAP) * (1 - is_lone)
         group = lax.div(late, 2 * CAP)
         low = pick(at_least(group, middle), group + 1, middle - group)
         high = pick(at_least(group, n_near), line + 1 + group - n_near, beyond + group)
         r = 2 * pick(at_least(line, 1), high, low) + lax.rem(late, 2)
         c = lax.div(lax.rem(late, 2 * CAP), 2)
-        return pick(is_late, r, me + 1), pick(is_late, c, n)
+        return pick(is_lone, me + 1, r), pick(is_lone, n - lone_at, c)
 
     def start_rows(b):
         acc[b] = jnp.zeros(acc.shape[1:], F32)
@@ -411,13 +413,14 @@
             cross_copy(step, i).wait_recv()
             fwd_copy(step, i).start()
 
-    def project(sources, places, tiles):
+    def weights_of(source, p):
+        return w[source * heads + lax.rem(p, heads)]
+
+    def project(i, sources, buffers):
+        places = [orders_of(source, at) for at in (i, i + 1) for source in sources]
+        tiles = [buffer(at) for at in (i, i + 1) for buffer in buffers]
         weights = jnp.concatenate(
-            [
-                w[source * heads + lax.rem(p, heads)]
-                for source, p in zip(sources, places)
-            ],
-            axis=0,
+            [weights_of(source, p) for source, p in zip(sources * 2, places)], axis=0
         )
         for b in range(blocks):
             seen = jnp.concatenate(
@@ -429,35 +432,64 @@
             )
             acc[b] += jnp.dot(seen, weights, preferred_element_type=F32)
 
-    def project_near(i):
-        near_copy(i).wait_recv()
-        project((hd, mate), (order[0, i], orders[mate, 0, i]), (own_g[i], mate_g[i]))
+    def orders_of(source, at):
+        return order[0, at] if source is hd else orders[source, 0, at]
 
     def project_far(i):
         for step in range(1, n_x):
-            fwd_copy(step, i).wait_recv()
             from_x = behind(step)
             from_mate = lax.rem(hx + n_x - step, n_x) * 2 + 1 - hc
-            project(
-                (from_x, from_mate),
-                (orders[from_x, 0, i], orders[from_mate, 0, i]),
-                (cross_g[step - 1, i], fwd_g[step - 1, i]),
+            fwd_copy(step, i).wait_recv()
+            fwd_copy(step, i + 1).wait_recv()
+            buffers = (lambda at: cross_g[step - 1, at], lambda at: fwd_g[step - 1, at])
+            project(i, (from_x, from_mate), buffers)
+
+    def project_beside(i):
+        near_copy(i).wait_recv()
+        near_copy(i + 1).wait_recv()
+        project(i, (hd, mate), (lambda at: own_g[at], lambda at: mate_g[at]))
+
+    beside = line >= middle
+
+    def project_near(b):
+        for tiles, source, where in (
+            (own_g, hd, lambda p: order[1, p]),
+            (mate_g, mate, lambda p: orders[mate, 1, p]),
+        ):
+            lined = jnp.concatenate(
+                [tiles[where(b * heads + h)] for h in range(heads)], axis=1
             )
+            weights = jnp.concatenate([w[source * heads + h] for h in range(heads)], axis=0)
+            acc[b] += jnp.dot(lined, weights, preferred_element_type=F32)
+
+    def end_near(i):
+        near_copy(i).wait_recv()
 
     def pass_on(i):
         forward(i)
-        project_near(i)
-
-        @pl.when(i > 0)
+
+        @pl.when((i > 0) & (lax.rem(i, 2) == 0))
         def _():
-            project_far(i - 1)
-
-    loop(0, free, lambda i: position(i, False))
+            project_far(i - 2)
+
+        @pl.when((i > 0) & (lax.rem(i, 2) == 0) & beside)
+        def _():
+            project_beside(i - 2)
+
+    early = jnp.where(line == 0, 4, jnp.where(line < middle, pairs, 2))
+
+    def placed(n):
+        return jnp.minimum(free, early + n + 1)
+
+    def free_step(i):
+        position(i, False)
+
+    loop(0, placed(-1), free_step)
     weight_load.wait()
     for d in range(1, n_head):
         order_wait(d).wait_recv()
 
-    n_late = jnp.where(line > 0, jnp.maximum(middle - line, 0) * 2 * CAP, 0)
+    n_late = jnp.where(line > 0, jnp.maximum(middle - line, 0), lines - 1 - middle) * 2 * CAP
     n_soon = n_serve - n_late
     ready = jnp.maximum(free - 1, 0)
 
@@ -466,16 +498,18 @@
 
     def soon_step(n):
         serve(n)
+        loop(placed(n - 1), placed(n), free_step)
         loop(passed(n - 1), passed(n), pass_on)
 
     loop(0, n_soon, soon_step)
+    loop(placed(n_soon - 1), free, free_step)
     start = passed(n_soon - 1)
 
     def gate(i):
         return jnp.maximum(n_tiles - (pairs - 1 - i), 0)
 
     def passed_gated(i):
-        return jnp.where((n_late > 0) | (i < free), start, jnp.maximum(i - 1, start))
+        return jnp.where(i < free, start, jnp.maximum(i - jnp.where(n_late > 0, 6, 2), start))
 
     def gated_step(i):
         loop(jnp.where(i == free, 0, gate(i - 1)), gate(i), take_tile)
@@ -495,9 +529,23 @@
 
     loop(n_soon, n_serve, late_step)
     loop(passed_late(n_serve - 1), pairs - 1, pass_on)
-    project_near(pairs - 1)
-    forward(pairs - 1)
-    loop(pairs - 2, pairs, project_far)
+    loop(jnp.where(beside, pairs, 0), pairs, end_near)
+
+    @pl.when(beside)
+    def _():
+        project_beside(pairs - 2)
+
+    def last_steps(b):
+        @pl.when(jnp.logical_not(beside))
+        def _():
+            project_near(b)
+
+        @pl.when(b == 0)
+        def _():
+            forward(pairs - 1)
+
+    loop(0, blocks, last_steps)
+    project_far(pairs - 2)
 
     def finish(b):
         out[pl.ds(pl.multiple_of(b * rows, rows), rows), :] = acc[b].astype(BF16)

time: 93.9 us -> 85.6 us (0.912)
  Pallas kernels: 90.6 us -> 82.3 us
    pallas_call x1, Pallas kernels: 90.6 us -> 82.3 us  [body(): pl.pallas_call(functools.partial(kernel, dims), out_shape=jax.ShapeDtypeS...]
where the time goes in v2:
time: 85.6 us; the launch traced here: 85.4 us
  Pallas kernels  82.3 us (96%)
  local copies, waits for them, and re-layouts  3.08 us (4%)
    pallas_call x1, Pallas kernels, body(): pl.pallas_call(functools.partial(kernel, dims), out_shape=jax.ShapeDtypeS...  82.3 us
    unnamed x1, local copies, waits for them, and re-layouts  3.08 us

profile of v2, /device:TPU:21, one launch (start us, length us, event | category | flops | bytes accessed | tf_op | source)
XLA Modules:
  0.0 85.4 jit_solution(1685335208534335774)
XLA Ops:
  0.0 82.3 %layer.1 = bf16[1024,1024]{1,0:T(8,128)(2,1)} custom-call(bf16[1024,1024]{1,0:T(8,128)(2,1)} %q_hbm.1, bf16[1024,1024]{1,0:T(8,128)(2,1)} %k_hbm.1, bf16[1024,1024]{1,0:T(8,128)(2,1)} %v_hbm.1, s32[2,4,8]{2,1,0:T(4,128)} %bitcast.3, bf16[32,128,1024]{2,1,0:T(8,128)(2,1)} %bitcast.2), custom_call_target="tpu_custom_call" | custom-call | tf_op jit(solution)/shard_map/layer/pallas_call | solution.py:597
  82.3 3.1 %copy.7 = bf16[1024,1024]{1,0:T(8,128)(2,1)} copy(bf16[1024,1024]{1,0:T(8,128)(2,1)} %layer.1) | data formatting | bytes 4194304
